TPU v7x, 32 devices: a whole 2x2x4 slice. The times are simulated.
32 devices in a mesh: curve: 8 (over z, x), level: 4 (over y, core).
Axes of the slice: x: 2, y: 2, z: 4, core: 2. Of those that a mesh axis runs over, the one named last changes fastest.
Arguments:
- right_side: float32 [512, 4096], P(None, ('curve', 'level')), may hold values from -6 to 6
- counts: int32 [32], replicated, may hold values from 96 to 128, as said below
- neighbours: int32 [6, 4096], P(None, ('curve', 'level')), may hold values from -1 to 4095, as said below
Outputs:
- solution: float32 [512, 4096], P(None, ('curve', 'level'))
- residual: float32 [512, 4096], P(None, ('curve', 'level'))
- residual_norm: float32 [], replicated
Inputs may be any that keep to these rules, and one draw needn't show every extreme that they name: `counts`: some device holds 128 live bricks and some device holds 96. `neighbours`: A slot's global number is its device times 128 plus its position. The relation is symmetric across opposite faces; padding slots have -1 on every face and no brick names them. Live bricks are numbered along the curve; the brick across face 0, 2 or 4 lies earlier on the curve and the one across face 1, 3 or 5 later, at most 256 live bricks away.
All inputs are finite; a program needn't handle non-finite values.
Results may differ from a plain program's by a relative error of at most 0.00027.
Values sent between devices are 32-bit elements; how exact they have to be, the bound alone decides.
A program may use at most 64 MiB of HBM per device.

v0:
```python
import jax
import jax.numpy as jnp
from jax import lax
from jax.sharding import PartitionSpec as P

MIN_LIVE = 96
LAYER = 256
HOPS = 3


OPPOSITE = (1, 0, 3, 2, 5, 4)
RELAXATION = 2.0 / 3.0


def from_behind(block, axis, distance):
    devices = range(lax.axis_size(axis))
    route = [(i - distance, i) for i in devices if i - distance in devices]
    return lax.ppermute(block, axis, route)


def brick_faces(values, extent):
    volume = values.reshape(extent, extent, extent, -1)
    surfaces = [
        volume[0],
        volume[extent - 1],
        volume[:, 0],
        volume[:, extent - 1],
        volume[:, :, 0],
        volume[:, :, extent - 1],
    ]
    return jnp.stack([one_face.reshape(extent * extent, -1) for one_face in surfaces])


def apply_operator(values, ghosts, extent, weight):
    brick_count = values.shape[1]
    volume = values.reshape(extent, extent, extent, brick_count)
    padded = jnp.pad(volume, ((1, 1), (1, 1), (1, 1), (0, 0)))
    shaped = [ghost.reshape(extent, extent, brick_count) for ghost in ghosts]
    padded = padded.at[0, 1:-1, 1:-1].set(shaped[0])
    padded = padded.at[-1, 1:-1, 1:-1].set(shaped[1])
    padded = padded.at[1:-1, 0, 1:-1].set(shaped[2])
    padded = padded.at[1:-1, -1, 1:-1].set(shaped[3])
    padded = padded.at[1:-1, 1:-1, 0].set(shaped[4])
    padded = padded.at[1:-1, 1:-1, -1].set(shaped[5])
    beside = padded[2:, 1:-1, 1:-1] + padded[:-2, 1:-1, 1:-1]
    beside = beside + padded[1:-1, 2:, 1:-1] + padded[1:-1, :-2, 1:-1]
    beside = beside + padded[1:-1, 1:-1, 2:] + padded[1:-1, 1:-1, :-2]
    return ((6.0 * volume - beside) * weight).reshape(extent * extent * extent, brick_count)


def restrict(values):
    brick_count = values.shape[1]
    grouped = values.reshape(4, 2, 4, 2, 4, 2, brick_count)
    return jnp.mean(grouped, axis=(1, 3, 5)).reshape(64, brick_count)


def prolong(coarse):
    brick_count = coarse.shape[1]
    spread = jnp.broadcast_to(
        coarse.reshape(4, 1, 4, 1, 4, 1, brick_count), (4, 2, 4, 2, 4, 2, brick_count)
    )
    return spread.reshape(512, brick_count)


def precondition(residual_in, exchange):
    relax_fine = RELAXATION / 6.0
    relax_coarse = RELAXATION / 1.5
    sweep_one = relax_fine * residual_in
    sweep_two = sweep_one + relax_fine * (
        residual_in - apply_operator(sweep_one, exchange(brick_faces(sweep_one, 8)), 8, 1.0)
    )
    defect = residual_in - apply_operator(sweep_two, exchange(brick_faces(sweep_two, 8)), 8, 1.0)
    coarse_rhs = restrict(defect)
    coarse_one = relax_coarse * coarse_rhs
    coarse_two = coarse_one + relax_coarse * (
        coarse_rhs - apply_operator(coarse_one, exchange(brick_faces(coarse_one, 4)), 4, 0.25)
    )
    sweep_three = sweep_two + prolong(coarse_two)
    return sweep_three + relax_fine * (
        residual_in - apply_operator(sweep_three, exchange(brick_faces(sweep_three, 8)), 8, 1.0)
    )


def local(right_side, counts, neighbours):
    slot_count = right_side.shape[1]
    device = lax.axis_index(("curve", "level"))
    own_count = counts[device]
    live_slot = jnp.arange(slot_count, dtype=jnp.int32) < own_count
    residual_in = jnp.where(live_slot[None, :], right_side, jnp.zeros_like(right_side))
    widths = [min(slot_count, LAYER - (hop - 1) * MIN_LIVE) for hop in range(1, HOPS + 1)]
    window_starts = []
    running = slot_count
    for width in widths:
        window_starts.append(running)
        running = running + width
    width_table = jnp.array(widths, dtype=jnp.int32)
    start_table = jnp.array(window_starts, dtype=jnp.int32)
    present = neighbours >= 0
    safe_slot = jnp.where(present, neighbours, 0)
    owner = safe_slot // slot_count
    offset = safe_slot % slot_count
    earlier = (jnp.arange(6, dtype=jnp.int32) % 2 == 0)[:, None]
    hop_index = jnp.clip(jnp.where(earlier, device - owner, owner - device), 1, HOPS) - 1
    skipped = jnp.where(earlier, jnp.maximum(counts[owner] - width_table[hop_index], 0), 0)
    position = jnp.where(owner == device, offset, start_table[hop_index] + offset - skipped)
    position = jnp.clip(jnp.where(present, position, 0), 0, running - 1)

    def exchange(surface):
        odd_faces = surface[1::2]
        even_faces = surface[0::2]
        lower = []
        upper = []
        for hop in range(1, HOPS + 1):
            width = widths[hop - 1]
            piece = lax.dynamic_slice_in_dim(odd_faces, jnp.maximum(own_count - width, 0), width, 2)
            lower.append(from_behind(piece, ("curve", "level"), hop))
            upper.append(from_behind(even_faces[:, :, :width], ("curve", "level"), -hop))
        ghosts = []
        for face_id in range(6):
            windows = lower if face_id % 2 == 0 else upper
            lookup = jnp.concatenate(
                [surface[OPPOSITE[face_id]]] + [window[face_id // 2] for window in windows], axis=1
            )
            picked = jnp.take(lookup, position[face_id], axis=1)
            ghosts.append(jnp.where(present[face_id][None, :], picked, jnp.zeros_like(picked)))
        return ghosts

    preconditioned = precondition(residual_in, exchange)
    image = apply_operator(preconditioned, exchange(brick_faces(preconditioned, 8)), 8, 1.0)
    local_along = jnp.sum(residual_in * preconditioned)
    local_curvature = jnp.sum(preconditioned * image)
    along, curvature, old_square, cross_term, image_square = lax.psum(
        (
            local_along,
            local_curvature,
            jnp.sum(residual_in * residual_in),
            jnp.sum(residual_in * image),
            jnp.sum(image * image),
        ),
        ("curve", "level"),
    )
    step_size = along / curvature
    solution = step_size * preconditioned
    residual = residual_in - step_size * image
    norm_square = old_square - 2.0 * step_size * cross_term + step_size * step_size * image_square
    return (solution, residual, jnp.sqrt(norm_square))


def solution(mesh):
    in_specs = (P(None, ("curve", "level")), P(), P(None, ("curve", "level")))
    out_specs = (P(None, ("curve", "level")), P(None, ("curve", "level")), P())
    return jax.shard_map(local, mesh=mesh, in_specs=in_specs, out_specs=out_specs, check_vma=False)
```

profile of v0, /device:TPU:0, one launch (start us, length us, event | category | flops | bytes accessed | tf_op | source)
XLA Modules:
  0.0 247.6 jit_solution(9839667775032948823)
XLA Ops:
  2.5 1.1 copy.169
  4.5 1.3 collective-permute-start.4
  5.8 1.3 collective-permute-start.3
  7.1 6.2 %collective-permute-start.1 = (f32[3,64,128]{1,2,0:T(8,128)S(1)}, f32[3,64,128]{1,2,0:T(8,128)S(1)}, u32[]{:S(2)}, u32[]{:S(2)}) collective-permute-start(f32[3,64,128]{1,2,0:T(8,128)S(1)} %get-tuple-element.404), channel_id=1, source_target_pairs={{0,2},{1,3},{2,4},{3,5},{4,6},{5,7},{6,8},{7,9},{8,10},{9,11},{10,... | collective-permute-start | bytes 294920 | tf_op jit(solution)/shard_map/ppermute | solution.py:18
  13.3 2.1 collective-permute-start
  16.1 5.5 %collective-permute-start.2 = (f32[3,64,64]{1,2,0:T(8,128)S(1)}, f32[3,64,64]{1,2,0:T(8,128)S(1)}, u32[]{:S(2)}, u32[]{:S(2)}) collective-permute-start(f32[3,64,64]{1,2,0:T(8,128)S(1)} %constant_dynamic-slice_fusion.4), channel_id=1, source_target_pairs={{0,3},{1,4},{2,5},{3,6},{4,7},{5,8},{6,9},{7,10},{8,11},{9,12},{10... | collective-permute-start | bytes 147464 | tf_op jit(solution)/shard_map/ppermute | solution.py:18
  23.0 4.8 %gather_fusion.1 = s32[768]{0:T(1024)S(1)} fusion(s32[32]{0:T(128)S(1)} %copy-done, s32[1024]{0:T(1024)S(1)} %get-tuple-element.555), kind=kCustom, calls=%fused_computation.31 | custom fusion | bytes 9216 | tf_op jit(solution)/shard_map/gather | solution.py:104
  28.5 4.8 %gather_fusion.2 = s32[768]{0:T(1024)S(1)} fusion(s32[3]{0:T(128)S(1)} %copy-done.2, s32[1024]{0:T(1024)S(1)} %get-tuple-element.556), kind=kCustom, calls=%fused_computation.32 | custom fusion | bytes 9216 | tf_op jit(solution)/shard_map/gather | solution.py:104
  33.3 4.8 %gather_fusion = s32[768]{0:T(1024)S(1)} fusion(s32[3]{0:T(128)S(1)} %copy-done.1, s32[1024]{0:T(1024)S(1)} %get-tuple-element.556), kind=kCustom, calls=%fused_computation.30 | custom fusion | bytes 9216 | tf_op jit(solution)/shard_map/gather | solution.py:105
  42.8 1.3 collective-permute-start.5
  44.1 4.6 %collective-permute-done.5 = f32[3,64,64]{1,2,0:T(8,128)S(1)} collective-permute-done((f32[3,64,64]{1,2,0:T(8,128)S(1)}, f32[3,64,64]{1,2,0:T(8,128)S(1)}, u32[]{:S(2)}, u32[]{:S(2)}) %collective-permute-start.5) | collective-permute-done | bytes 49184 | tf_op jit(solution)/shard_map/ppermute | solution.py:18
  49.6 0.8 gather_fusion.4
  51.9 0.8 gather_fusion.6
  53.7 0.8 gather_fusion.7
  56.3 0.8 gather_fusion.5
  60.4 3.3 %collective-permute-start.8 = (f32[3,64,64]{1,2,0:T(8,128)S(1)}, f32[3,64,64]{1,2,0:T(8,128)S(1)}, u32[]{:S(2)}, u32[]{:S(2)}) collective-permute-start(f32[3,64,64]{1,2,0:T(8,128)S(1)} %constant_dynamic-slice_fusion.3), channel_id=1, source_target_pairs={{0,3},{1,4},{2,5},{3,6},{4,7},{5,8},{6,9},{7,10},{8,11},{9,12},{10... | collective-permute-start | bytes 147464 | tf_op jit(solution)/shard_map/ppermute | solution.py:18
  63.8 1.3 collective-permute-start.10
  65.1 1.3 collective-permute-start.9
  66.4 5.4 %collective-permute-start.7 = (f32[3,64,128]{1,2,0:T(8,128)S(1)}, f32[3,64,128]{1,2,0:T(8,128)S(1)}, u32[]{:S(2)}, u32[]{:S(2)}) collective-permute-start(f32[3,64,128]{1,2,0:T(8,128)S(1)} %get-tuple-element.402), channel_id=1, source_target_pairs={{0,2},{1,3},{2,4},{3,5},{4,6},{5,7},{6,8},{7,9},{8,10},{9,11},{10,... | collective-permute-start | bytes 294920 | tf_op jit(solution)/shard_map/ppermute | solution.py:18
  71.9 3.3 %collective-permute-start.6 = (f32[3,64,128]{1,2,0:T(8,128)S(1)}, f32[3,64,128]{1,2,0:T(8,128)S(1)}, u32[]{:S(2)}, u32[]{:S(2)}) collective-permute-start(f32[3,64,128]{1,2,0:T(8,128)S(1)} %get-tuple-element.402), channel_id=1, source_target_pairs={{0,1},{1,2},{2,3},{3,4},{4,5},{5,6},{6,7},{7,8},{8,9},{9,10},{10,1... | collective-permute-start | bytes 294920 | tf_op jit(solution)/shard_map/ppermute | solution.py:18
  75.6 1.3 collective-permute-start.11
  77.6 6.5 %collective-permute-done.11 = f32[3,64,64]{1,2,0:T(8,128)S(1)} collective-permute-done((f32[3,64,64]{1,2,0:T(8,128)S(1)}, f32[3,64,64]{1,2,0:T(8,128)S(1)}, u32[]{:S(2)}, u32[]{:S(2)}) %collective-permute-start.11) | collective-permute-done | bytes 49184 | tf_op jit(solution)/shard_map/ppermute | solution.py:18
  84.8 0.9 gather_fusion.14
  86.5 0.8 gather_fusion.12
  88.1 0.8 gather_fusion.10
  90.7 0.8 gather_fusion.13
  97.2 3.9 %collective-permute-start.14 = (f32[3,16,64]{2,1,0:T(8,128)S(1)}, f32[3,16,64]{2,1,0:T(8,128)S(1)}, u32[]{:S(2)}, u32[]{:S(2)}) collective-permute-start(f32[3,16,64]{2,1,0:T(8,128)S(1)} %constant_dynamic-slice_fusion.2), channel_id=1, source_target_pairs={{0,3},{1,4},{2,5},{3,6},{4,7},{5,8},{6,9},{7,10},{8,11},{9,12},{10... | collective-permute-start | bytes 36872 | tf_op jit(solution)/shard_map/ppermute | solution.py:18
  101.1 1.3 collective-permute-start.16
  102.4 1.3 collective-permute-start.15
  103.7 6.0 %collective-permute-start.13 = (f32[3,16,128]{2,1,0:T(8,128)S(1)}, f32[3,16,128]{2,1,0:T(8,128)S(1)}, u32[]{:S(2)}, u32[]{:S(2)}) collective-permute-start(f32[3,16,128]{2,1,0:T(8,128)S(1)} %get-tuple-element.510), channel_id=1, source_target_pairs={{0,2},{1,3},{2,4},{3,5},{4,6},{5,7},{6,8},{7,9},{8,10},{9,11},{10,... | collective-permute-start | bytes 73736 | tf_op jit(solution)/shard_map/ppermute | solution.py:18
  109.7 2.1 collective-permute-start.12
  111.9 1.3 collective-permute-start.17
  113.2 5.7 %collective-permute-done.17 = f32[3,16,64]{2,1,0:T(8,128)S(1)} collective-permute-done((f32[3,16,64]{2,1,0:T(8,128)S(1)}, f32[3,16,64]{2,1,0:T(8,128)S(1)}, u32[]{:S(2)}, u32[]{:S(2)}) %collective-permute-start.17) | collective-permute-done | bytes 12320 | tf_op jit(solution)/shard_map/ppermute | solution.py:18
  120.1 0.8 gather_fusion.17
  121.1 0.8 gather_fusion.19
  122.4 0.8 gather_fusion.16
  123.5 0.8 gather_fusion.18
  124.6 0.8 gather_fusion.20
  127.3 3.9 %collective-permute-start.20 = (f32[3,64,64]{1,2,0:T(8,128)S(1)}, f32[3,64,64]{1,2,0:T(8,128)S(1)}, u32[]{:S(2)}, u32[]{:S(2)}) collective-permute-start(f32[3,64,64]{1,2,0:T(8,128)S(1)} %constant_dynamic-slice_fusion.1), channel_id=1, source_target_pairs={{0,3},{1,4},{2,5},{3,6},{4,7},{5,8},{6,9},{7,10},{8,11},{9,12},{10... | collective-permute-start | bytes 147464 | tf_op jit(solution)/shard_map/ppermute | solution.py:18
  131.3 1.3 collective-permute-start.22
  132.6 1.3 collective-permute-start.21
  133.9 6.2 %collective-permute-start.19 = (f32[3,64,128]{1,2,0:T(8,128)S(1)}, f32[3,64,128]{1,2,0:T(8,128)S(1)}, u32[]{:S(2)}, u32[]{:S(2)}) collective-permute-start(f32[3,64,128]{1,2,0:T(8,128)S(1)} %get-tuple-element.400), channel_id=1, source_target_pairs={{0,2},{1,3},{2,4},{3,5},{4,6},{5,7},{6,8},{7,9},{8,10},{9,11},{10,... | collective-permute-start | bytes 294920 | tf_op jit(solution)/shard_map/ppermute | solution.py:18
  140.1 2.1 collective-permute-start.18
  142.8 1.5 collective-permute-start.23
  144.9 5.7 %collective-permute-done.23 = f32[3,64,64]{1,2,0:T(8,128)S(1)} collective-permute-done((f32[3,64,64]{1,2,0:T(8,128)S(1)}, f32[3,64,64]{1,2,0:T(8,128)S(1)}, u32[]{:S(2)}, u32[]{:S(2)}) %collective-permute-start.23) | collective-permute-done | bytes 49184 | tf_op jit(solution)/shard_map/ppermute | solution.py:18
  151.3 0.9 gather_fusion.26
  153.0 0.8 gather_fusion.24
  154.6 0.8 gather_fusion.22
  157.2 0.8 gather_fusion.25
  164.1 1.3 collective-permute-start.28
  165.4 1.3 collective-permute-start.27
  166.7 1.3 collective-permute-start.29
  168.7 5.5 %collective-permute-start.25 = (f32[3,64,128]{1,2,0:T(8,128)S(1)}, f32[3,64,128]{1,2,0:T(8,128)S(1)}, u32[]{:S(2)}, u32[]{:S(2)}) collective-permute-start(f32[3,64,128]{1,2,0:T(8,128)S(1)} %get-tuple-element.398), channel_id=1, source_target_pairs={{0,2},{1,3},{2,4},{3,5},{4,6},{5,7},{6,8},{7,9},{8,10},{9,11},{10,... | collective-permute-start | bytes 294920 | tf_op jit(solution)/shard_map/ppermute | solution.py:18
  174.2 3.0 %collective-permute-start.24 = (f32[3,64,128]{1,2,0:T(8,128)S(1)}, f32[3,64,128]{1,2,0:T(8,128)S(1)}, u32[]{:S(2)}, u32[]{:S(2)}) collective-permute-start(f32[3,64,128]{1,2,0:T(8,128)S(1)} %get-tuple-element.398), channel_id=1, source_target_pairs={{0,1},{1,2},{2,3},{3,4},{4,5},{5,6},{6,7},{7,8},{8,9},{9,10},{10,1... | collective-permute-start | bytes 294920 | tf_op jit(solution)/shard_map/ppermute | solution.py:18
  177.7 5.5 %collective-permute-start.26 = (f32[3,64,64]{1,2,0:T(8,128)}, f32[3,64,64]{1,2,0:T(8,128)S(1)}, u32[]{:S(2)}, u32[]{:S(2)}) collective-permute-start(f32[3,64,64]{1,2,0:T(8,128)} %constant_dynamic-slice_fusion), channel_id=1, source_target_pairs={{0,3},{1,4},{2,5},{3,6},{4,7},{5,8},{6,9},{7,10},{8,11},{9,12},{10... | collective-permute-start | bytes 147464 | tf_op jit(solution)/shard_map/ppermute | solution.py:18
  183.8 1.9 collective-permute-done.26
  186.4 0.9 gather_fusion.32
  188.1 0.8 gather_fusion.30
  189.7 0.8 gather_fusion.28
  192.3 0.8 gather_fusion.31
  197.4 0.8 multiply_reduce_fusion.1
  198.2 43.2 %all-reduce.5 = (f32[]{:T(128)}, f32[]{:T(128)}, f32[]{:T(128)}, f32[]{:T(128)}, f32[]{:T(128)}) all-reduce(f32[]{:T(128)} %get-tuple-element.375, f32[]{:T(128)} %get-tuple-element.376, f32[]{:T(128)} %get-tuple-element.377, f32[]{:T(128)} %get-tuple-element.374, ...), channel_id=1, replica_groups=mesh['curve'=8,'level'=4] {'curve','level'}, use_global_device_ids=true, to_apply=%region_2.5 | all-reduce | flops 5 | bytes 40 | tf_op jit(solution)/shard_map/psum | solution.py:132
  244.8 0.8 copy.270
  245.6 0.8 copy.271
  (444 shorter events, 53.6 us)
Async XLA Ops:
  2.5 1.1 copy-start.55
  4.5 44.2 %collective-permute-start.4 = (f32[3,64,128]{1,2,0:T(8,128)S(1)}, f32[3,64,128]{1,2,0:T(8,128)S(1)}, u32[]{:S(2)}, u32[]{:S(2)}) collective-permute-start(f32[3,64,128]{1,2,0:T(8,128)S(1)} %get-tuple-element.403), channel_id=1, source_target_pairs={{2,0},{3,1},{4,2},{5,3},{6,4},{7,5},{8,6},{9,7},{10,8},{11,9},{12,... | collective-permute-start | bytes 294920 | tf_op jit(solution)/shard_map/ppermute | solution.py:18
  5.8 42.9 %collective-permute-start.3 = (f32[3,64,128]{1,2,0:T(8,128)S(1)}, f32[3,64,128]{1,2,0:T(8,128)S(1)}, u32[]{:S(2)}, u32[]{:S(2)}) collective-permute-start(f32[3,64,128]{1,2,0:T(8,128)S(1)} %get-tuple-element.403), channel_id=1, source_target_pairs={{1,0},{2,1},{3,2},{4,3},{5,4},{6,5},{7,6},{8,7},{9,8},{10,9},{11,1... | collective-permute-start | bytes 294920 | tf_op jit(solution)/shard_map/ppermute | solution.py:18
  7.1 45.5 %collective-permute-start.1 = (f32[3,64,128]{1,2,0:T(8,128)S(1)}, f32[3,64,128]{1,2,0:T(8,128)S(1)}, u32[]{:S(2)}, u32[]{:S(2)}) collective-permute-start(f32[3,64,128]{1,2,0:T(8,128)S(1)} %get-tuple-element.404), channel_id=1, source_target_pairs={{0,2},{1,3},{2,4},{3,5},{4,6},{5,7},{6,8},{7,9},{8,10},{9,11},{10,... | collective-permute-start | bytes 294920 | tf_op jit(solution)/shard_map/ppermute | solution.py:18
  13.3 40.3 %collective-permute-start = (f32[3,64,128]{1,2,0:T(8,128)S(1)}, f32[3,64,128]{1,2,0:T(8,128)S(1)}, u32[]{:S(2)}, u32[]{:S(2)}) collective-permute-start(f32[3,64,128]{1,2,0:T(8,128)S(1)} %get-tuple-element.404), channel_id=1, source_target_pairs={{0,1},{1,2},{2,3},{3,4},{4,5},{5,6},{6,7},{7,8},{8,9},{9,10},{10,1... | collective-permute-start | bytes 294920 | tf_op jit(solution)/shard_map/ppermute | solution.py:18
  16.1 26.6 %collective-permute-start.2 = (f32[3,64,64]{1,2,0:T(8,128)S(1)}, f32[3,64,64]{1,2,0:T(8,128)S(1)}, u32[]{:S(2)}, u32[]{:S(2)}) collective-permute-start(f32[3,64,64]{1,2,0:T(8,128)S(1)} %constant_dynamic-slice_fusion.4), channel_id=1, source_target_pairs={{0,3},{1,4},{2,5},{3,6},{4,7},{5,8},{6,9},{7,10},{8,11},{9,12},{10... | collective-permute-start | bytes 147464 | tf_op jit(solution)/shard_map/ppermute | solution.py:18
  28.5 4.8 %copy-start.1 = (s32[3]{0:T(128)S(1)}, s32[3]{0:T(128)}, u32[]{:S(2)}) copy-start(s32[3]{0:T(128)} %constant.873.clone) | copy-start | bytes 40
  38.7 12.5 %copy-start.43 = (pred[128]{0:T(512)(128)(4,1)}, pred[128]{0:T(512)(128)(4,1)S(1)}, u32[]{:S(2)}) copy-start(pred[128]{0:T(512)(128)(4,1)S(1)} %get-tuple-element.541) | copy-start | bytes 388
  38.7 56.1 %copy-start.20 = (pred[128]{0:T(512)(128)(4,1)}, pred[128]{0:T(512)(128)(4,1)S(1)}, u32[]{:S(2)}) copy-start(pred[128]{0:T(512)(128)(4,1)S(1)} %get-tuple-element.543) | copy-start | bytes 388
  42.8 5.9 %collective-permute-start.5 = (f32[3,64,64]{1,2,0:T(8,128)S(1)}, f32[3,64,64]{1,2,0:T(8,128)S(1)}, u32[]{:S(2)}, u32[]{:S(2)}) collective-permute-start(f32[3,64,64]{1,2,0:T(8,128)S(1)} %slice.1835), channel_id=1, source_target_pairs={{3,0},{4,1},{5,2},{6,3},{7,4},{8,5},{9,6},{10,7},{11,8},{12,9},{13... | collective-permute-start | bytes 147464 | tf_op jit(solution)/shard_map/ppermute | solution.py:18
  60.4 15.2 %collective-permute-start.8 = (f32[3,64,64]{1,2,0:T(8,128)S(1)}, f32[3,64,64]{1,2,0:T(8,128)S(1)}, u32[]{:S(2)}, u32[]{:S(2)}) collective-permute-start(f32[3,64,64]{1,2,0:T(8,128)S(1)} %constant_dynamic-slice_fusion.3), channel_id=1, source_target_pairs={{0,3},{1,4},{2,5},{3,6},{4,7},{5,8},{6,9},{7,10},{8,11},{9,12},{10... | collective-permute-start | bytes 147464 | tf_op jit(solution)/shard_map/ppermute | solution.py:18
  63.8 20.9 %collective-permute-start.10 = (f32[3,64,128]{1,2,0:T(8,128)S(1)}, f32[3,64,128]{1,2,0:T(8,128)S(1)}, u32[]{:S(2)}, u32[]{:S(2)}) collective-permute-start(f32[3,64,128]{1,2,0:T(8,128)S(1)} %get-tuple-element.401), channel_id=1, source_target_pairs={{2,0},{3,1},{4,2},{5,3},{6,4},{7,5},{8,6},{9,7},{10,8},{11,9},{12,... | collective-permute-start | bytes 294920 | tf_op jit(solution)/shard_map/ppermute | solution.py:18
  65.1 19.6 %collective-permute-start.9 = (f32[3,64,128]{1,2,0:T(8,128)S(1)}, f32[3,64,128]{1,2,0:T(8,128)S(1)}, u32[]{:S(2)}, u32[]{:S(2)}) collective-permute-start(f32[3,64,128]{1,2,0:T(8,128)S(1)} %get-tuple-element.401), channel_id=1, source_target_pairs={{1,0},{2,1},{3,2},{4,3},{5,4},{6,5},{7,6},{8,7},{9,8},{10,9},{11,1... | collective-permute-start | bytes 294920 | tf_op jit(solution)/shard_map/ppermute | solution.py:18
  66.4 22.4 %collective-permute-start.7 = (f32[3,64,128]{1,2,0:T(8,128)S(1)}, f32[3,64,128]{1,2,0:T(8,128)S(1)}, u32[]{:S(2)}, u32[]{:S(2)}) collective-permute-start(f32[3,64,128]{1,2,0:T(8,128)S(1)} %get-tuple-element.402), channel_id=1, source_target_pairs={{0,2},{1,3},{2,4},{3,5},{4,6},{5,7},{6,8},{7,9},{8,10},{9,11},{10,... | collective-permute-start | bytes 294920 | tf_op jit(solution)/shard_map/ppermute | solution.py:18
  71.9 18.1 %collective-permute-start.6 = (f32[3,64,128]{1,2,0:T(8,128)S(1)}, f32[3,64,128]{1,2,0:T(8,128)S(1)}, u32[]{:S(2)}, u32[]{:S(2)}) collective-permute-start(f32[3,64,128]{1,2,0:T(8,128)S(1)} %get-tuple-element.402), channel_id=1, source_target_pairs={{0,1},{1,2},{2,3},{3,4},{4,5},{5,6},{6,7},{7,8},{8,9},{9,10},{10,1... | collective-permute-start | bytes 294920 | tf_op jit(solution)/shard_map/ppermute | solution.py:18
  75.6 8.4 %collective-permute-start.11 = (f32[3,64,64]{1,2,0:T(8,128)S(1)}, f32[3,64,64]{1,2,0:T(8,128)S(1)}, u32[]{:S(2)}, u32[]{:S(2)}) collective-permute-start(f32[3,64,64]{1,2,0:T(8,128)S(1)} %slice.1866), channel_id=1, source_target_pairs={{3,0},{4,1},{5,2},{6,3},{7,4},{8,5},{9,6},{10,7},{11,8},{12,9},{13... | collective-permute-start | bytes 147464 | tf_op jit(solution)/shard_map/ppermute | solution.py:18
  84.8 0.9 copy-start.40
  84.8 0.9 copy-start.52
  86.5 0.8 copy-start.36
  86.5 0.8 copy-start.48
  89.9 0.8 copy-start.7
  90.7 0.8 copy-start.32
  91.6 0.8 copy-start.5
  92.4 0.8 copy-start.24
  93.2 0.8 copy-start.3
  97.2 14.7 %collective-permute-start.14 = (f32[3,16,64]{2,1,0:T(8,128)S(1)}, f32[3,16,64]{2,1,0:T(8,128)S(1)}, u32[]{:S(2)}, u32[]{:S(2)}) collective-permute-start(f32[3,16,64]{2,1,0:T(8,128)S(1)} %constant_dynamic-slice_fusion.2), channel_id=1, source_target_pairs={{0,3},{1,4},{2,5},{3,6},{4,7},{5,8},{6,9},{7,10},{8,11},{9,12},{10... | collective-permute-start | bytes 36872 | tf_op jit(solution)/shard_map/ppermute | solution.py:18
  101.1 20.9 %collective-permute-start.16 = (f32[3,16,128]{2,1,0:T(8,128)S(1)}, f32[3,16,128]{2,1,0:T(8,128)S(1)}, u32[]{:S(2)}, u32[]{:S(2)}) collective-permute-start(f32[3,16,128]{2,1,0:T(8,128)S(1)} %get-tuple-element.509), channel_id=1, source_target_pairs={{2,0},{3,1},{4,2},{5,3},{6,4},{7,5},{8,6},{9,7},{10,8},{11,9},{12,... | collective-permute-start | bytes 73736 | tf_op jit(solution)/shard_map/ppermute | solution.py:18
  102.4 19.8 %collective-permute-start.15 = (f32[3,16,128]{2,1,0:T(8,128)S(1)}, f32[3,16,128]{2,1,0:T(8,128)S(1)}, u32[]{:S(2)}, u32[]{:S(2)}) collective-permute-start(f32[3,16,128]{2,1,0:T(8,128)S(1)} %get-tuple-element.509), channel_id=1, source_target_pairs={{1,0},{2,1},{3,2},{4,3},{5,4},{6,5},{7,6},{8,7},{9,8},{10,9},{11,1... | collective-permute-start | bytes 73736 | tf_op jit(solution)/shard_map/ppermute | solution.py:18
  103.7 15.2 %collective-permute-start.13 = (f32[3,16,128]{2,1,0:T(8,128)S(1)}, f32[3,16,128]{2,1,0:T(8,128)S(1)}, u32[]{:S(2)}, u32[]{:S(2)}) collective-permute-start(f32[3,16,128]{2,1,0:T(8,128)S(1)} %get-tuple-element.510), channel_id=1, source_target_pairs={{0,2},{1,3},{2,4},{3,5},{4,6},{5,7},{6,8},{7,9},{8,10},{9,11},{10,... | collective-permute-start | bytes 73736 | tf_op jit(solution)/shard_map/ppermute | solution.py:18
  109.7 9.2 %collective-permute-start.12 = (f32[3,16,128]{2,1,0:T(8,128)S(1)}, f32[3,16,128]{2,1,0:T(8,128)S(1)}, u32[]{:S(2)}, u32[]{:S(2)}) collective-permute-start(f32[3,16,128]{2,1,0:T(8,128)S(1)} %get-tuple-element.510), channel_id=1, source_target_pairs={{0,1},{1,2},{2,3},{3,4},{4,5},{5,6},{6,7},{7,8},{8,9},{9,10},{10,1... | collective-permute-start | bytes 73736 | tf_op jit(solution)/shard_map/ppermute | solution.py:18
  111.9 7.0 %collective-permute-start.17 = (f32[3,16,64]{2,1,0:T(8,128)S(1)}, f32[3,16,64]{2,1,0:T(8,128)S(1)}, u32[]{:S(2)}, u32[]{:S(2)}) collective-permute-start(f32[3,16,64]{2,1,0:T(8,128)S(1)} %bitcast.526), channel_id=1, source_target_pairs={{3,0},{4,1},{5,2},{6,3},{7,4},{8,5},{9,6},{10,7},{11,8},{12,9},{13... | collective-permute-start | bytes 36872 | tf_op jit(solution)/shard_map/ppermute | solution.py:18
  119.1 0.8 copy-start.21
  121.1 0.8 copy-start.18
  127.3 15.5 %collective-permute-start.20 = (f32[3,64,64]{1,2,0:T(8,128)S(1)}, f32[3,64,64]{1,2,0:T(8,128)S(1)}, u32[]{:S(2)}, u32[]{:S(2)}) collective-permute-start(f32[3,64,64]{1,2,0:T(8,128)S(1)} %constant_dynamic-slice_fusion.1), channel_id=1, source_target_pairs={{0,3},{1,4},{2,5},{3,6},{4,7},{5,8},{6,9},{7,10},{8,11},{9,12},{10... | collective-permute-start | bytes 147464 | tf_op jit(solution)/shard_map/ppermute | solution.py:18
  131.3 19.8 %collective-permute-start.22 = (f32[3,64,128]{1,2,0:T(8,128)S(1)}, f32[3,64,128]{1,2,0:T(8,128)S(1)}, u32[]{:S(2)}, u32[]{:S(2)}) collective-permute-start(f32[3,64,128]{1,2,0:T(8,128)S(1)} %get-tuple-element.399), channel_id=1, source_target_pairs={{2,0},{3,1},{4,2},{5,3},{6,4},{7,5},{8,6},{9,7},{10,8},{11,9},{12,... | collective-permute-start | bytes 294920 | tf_op jit(solution)/shard_map/ppermute | solution.py:18
  132.6 18.6 %collective-permute-start.21 = (f32[3,64,128]{1,2,0:T(8,128)S(1)}, f32[3,64,128]{1,2,0:T(8,128)S(1)}, u32[]{:S(2)}, u32[]{:S(2)}) collective-permute-start(f32[3,64,128]{1,2,0:T(8,128)S(1)} %get-tuple-element.399), channel_id=1, source_target_pairs={{1,0},{2,1},{3,2},{4,3},{5,4},{6,5},{7,6},{8,7},{9,8},{10,9},{11,1... | collective-permute-start | bytes 294920 | tf_op jit(solution)/shard_map/ppermute | solution.py:18
  133.9 21.4 %collective-permute-start.19 = (f32[3,64,128]{1,2,0:T(8,128)S(1)}, f32[3,64,128]{1,2,0:T(8,128)S(1)}, u32[]{:S(2)}, u32[]{:S(2)}) collective-permute-start(f32[3,64,128]{1,2,0:T(8,128)S(1)} %get-tuple-element.400), channel_id=1, source_target_pairs={{0,2},{1,3},{2,4},{3,5},{4,6},{5,7},{6,8},{7,9},{8,10},{9,11},{10,... | collective-permute-start | bytes 294920 | tf_op jit(solution)/shard_map/ppermute | solution.py:18
  140.1 16.2 %collective-permute-start.18 = (f32[3,64,128]{1,2,0:T(8,128)S(1)}, f32[3,64,128]{1,2,0:T(8,128)S(1)}, u32[]{:S(2)}, u32[]{:S(2)}) collective-permute-start(f32[3,64,128]{1,2,0:T(8,128)S(1)} %get-tuple-element.400), channel_id=1, source_target_pairs={{0,1},{1,2},{2,3},{3,4},{4,5},{5,6},{6,7},{7,8},{8,9},{9,10},{10,1... | collective-permute-start | bytes 294920 | tf_op jit(solution)/shard_map/ppermute | solution.py:18
  142.8 7.8 %collective-permute-start.23 = (f32[3,64,64]{1,2,0:T(8,128)S(1)}, f32[3,64,64]{1,2,0:T(8,128)S(1)}, u32[]{:S(2)}, u32[]{:S(2)}) collective-permute-start(f32[3,64,64]{1,2,0:T(8,128)S(1)} %slice.1928), channel_id=1, source_target_pairs={{3,0},{4,1},{5,2},{6,3},{7,4},{8,5},{9,6},{10,7},{11,8},{12,9},{13... | collective-permute-start | bytes 147464 | tf_op jit(solution)/shard_map/ppermute | solution.py:18
  151.3 0.9 copy-start.41
  151.3 0.9 copy-start.53
  152.2 0.8 copy-start.15
  153.0 0.8 copy-start.37
  153.0 0.8 copy-start.49
  156.4 0.8 copy-start.8
  157.2 0.8 copy-start.19
  157.2 0.8 copy-start.33
  158.1 0.8 copy-start.6
  158.9 0.8 copy-start.25
  160.5 0.8 copy-start.22
  164.1 22.2 %collective-permute-start.28 = (f32[3,64,128]{1,2,0:T(8,128)S(1)}, f32[3,64,128]{1,2,0:T(8,128)S(1)}, u32[]{:S(2)}, u32[]{:S(2)}) collective-permute-start(f32[3,64,128]{1,2,0:T(8,128)S(1)} %get-tuple-element.397), channel_id=1, source_target_pairs={{2,0},{3,1},{4,2},{5,3},{6,4},{7,5},{8,6},{9,7},{10,8},{11,9},{12,... | collective-permute-start | bytes 294920 | tf_op jit(solution)/shard_map/ppermute | solution.py:18
  165.4 20.9 %collective-permute-start.27 = (f32[3,64,128]{1,2,0:T(8,128)S(1)}, f32[3,64,128]{1,2,0:T(8,128)S(1)}, u32[]{:S(2)}, u32[]{:S(2)}) collective-permute-start(f32[3,64,128]{1,2,0:T(8,128)S(1)} %get-tuple-element.397), channel_id=1, source_target_pairs={{1,0},{2,1},{3,2},{4,3},{5,4},{6,5},{7,6},{8,7},{9,8},{10,9},{11,1... | collective-permute-start | bytes 294920 | tf_op jit(solution)/shard_map/ppermute | solution.py:18
  166.7 11.0 %collective-permute-start.29 = (f32[3,64,64]{1,2,0:T(8,128)S(1)}, f32[3,64,64]{1,2,0:T(8,128)S(1)}, u32[]{:S(2)}, u32[]{:S(2)}) collective-permute-start(f32[3,64,64]{1,2,0:T(8,128)S(1)} %slice.1959), channel_id=1, source_target_pairs={{3,0},{4,1},{5,2},{6,3},{7,4},{8,5},{9,6},{10,7},{11,8},{12,9},{13... | collective-permute-start | bytes 147464 | tf_op jit(solution)/shard_map/ppermute | solution.py:18
  168.7 21.8 %collective-permute-start.25 = (f32[3,64,128]{1,2,0:T(8,128)S(1)}, f32[3,64,128]{1,2,0:T(8,128)S(1)}, u32[]{:S(2)}, u32[]{:S(2)}) collective-permute-start(f32[3,64,128]{1,2,0:T(8,128)S(1)} %get-tuple-element.398), channel_id=1, source_target_pairs={{0,2},{1,3},{2,4},{3,5},{4,6},{5,7},{6,8},{7,9},{8,10},{9,11},{10,... | collective-permute-start | bytes 294920 | tf_op jit(solution)/shard_map/ppermute | solution.py:18
  174.2 17.3 %collective-permute-start.24 = (f32[3,64,128]{1,2,0:T(8,128)S(1)}, f32[3,64,128]{1,2,0:T(8,128)S(1)}, u32[]{:S(2)}, u32[]{:S(2)}) collective-permute-start(f32[3,64,128]{1,2,0:T(8,128)S(1)} %get-tuple-element.398), channel_id=1, source_target_pairs={{0,1},{1,2},{2,3},{3,4},{4,5},{5,6},{6,7},{7,8},{8,9},{9,10},{10,1... | collective-permute-start | bytes 294920 | tf_op jit(solution)/shard_map/ppermute | solution.py:18
  177.7 8.0 %collective-permute-start.26 = (f32[3,64,64]{1,2,0:T(8,128)}, f32[3,64,64]{1,2,0:T(8,128)S(1)}, u32[]{:S(2)}, u32[]{:S(2)}) collective-permute-start(f32[3,64,64]{1,2,0:T(8,128)} %constant_dynamic-slice_fusion), channel_id=1, source_target_pairs={{0,3},{1,4},{2,5},{3,6},{4,7},{5,8},{6,9},{7,10},{8,11},{9,12},{10... | collective-permute-start | bytes 147464 | tf_op jit(solution)/shard_map/ppermute | solution.py:18
  186.4 0.9 copy-start.42
  186.4 0.9 copy-start.54
  187.3 0.8 copy-start.11
  188.1 0.8 copy-start.38
  188.1 0.8 copy-start.50
  191.5 0.8 copy-start.9
  192.3 0.8 copy-start.34
  193.3 0.8 copy-start.26
  (26 other events, 16.9 us)
where the time goes:
time: 250 us; the launch traced here: 248 us
  starting transfers between devices  83.7 us (33%)
  local copies, waits for them, and re-layouts  76.8 us (31%)
  blocking collectives  43.2 us (17%)
  waiting for transfers between devices  24.4 us (10%)
  other arithmetic  11.1 us (4%)
  between operations  8.26 us (3%)
    ppermute x30, starting transfers between devices, from_behind(): return lax.ppermute(block, axis, route)  83.7 us
    psum x1, blocking collectives, local(): lax.psum((local_along, local_curvature, jnp.sum(residual_in * residual_in...  43.2 us
    ppermute x30, waiting for transfers between devices, from_behind(): return lax.ppermute(block, axis, route)  24.4 us
    gather x30, local copies, waits for them, and re-layouts, exchange(): picked = jnp.take(lookup, position[face_id], axis=1)  23.5 us
    unnamed x148, local copies, waits for them, and re-layouts  20.8 us
  transfers between devices with their start and end apart: 30, of which 5 were waited for; matrix products, arithmetic and copies ran while one was open for 17% of the time, Pallas kernels for 0%

commit v1 on v0

v1 whole, which is shorter than its diff:
```python
import functools

import jax
import jax.numpy as jnp
from jax import lax
from jax.experimental import pallas as pl
from jax.experimental.pallas import tpu as pltpu
from jax.sharding import PartitionSpec as P

MIN_LIVE = 96
LAYER = 256
HOPS = 3
AXES = ("curve", "level")
MESH = pl.DeviceIdType.MESH
RELAXATION = 2.0 / 3.0
RELAX_FINE = RELAXATION / 6.0
RELAX_COARSE = RELAXATION / 1.5
F32 = jnp.float32


def kernel(
    sizes,
    stages,
    right_ref,
    counts_ref,
    neighbours_ref,
    solution_ref,
    residual_ref,
    norm_ref,
    source,
    first,
    second,
    image,
    zghost,
    paired,
    coarse,
    shifted,
    faces_fine,
    packed_fine,
    near_fine,
    far_fine,
    faces_coarse,
    packed_coarse,
    near_coarse,
    far_coarse,
    sums,
    send_sems,
    recv_sems,
    sum_send,
    sum_recv,
):
    curve_size, level_size = sizes
    total = curve_size * level_size
    me = lax.axis_index("curve") * level_size + lax.axis_index("level")
    lanes = right_ref.shape[1]
    half = lanes // 2

    def place(index):
        return (index // level_size, index % level_size)

    barrier = pltpu.get_barrier_semaphore()
    greeted = 0
    for size, _, partner in stages:
        for k in range(1, size):
            pl.semaphore_signal(barrier, inc=1, device_id=partner(k), device_id_type=MESH)
            greeted += 1
    direct = len(stages) == 1
    if not direct:
        for hop in range(1, HOPS + 1):
            for sign in (1, -1):
                target = (me + sign * hop + total) % total
                pl.semaphore_signal(barrier, inc=1, device_id=place(target), device_id_type=MESH)
                greeted += 1

    lane = lax.broadcasted_iota(jnp.int32, (1, lanes), 1)
    own_count = counts_ref[me]
    live = lane < own_count
    for x in range(8):
        rows = pl.ds(64 * x, 64)
        value = jnp.where(live, right_ref[rows, :], 0.0)
        source[rows, :] = value
        first[rows, :] = RELAX_FINE * value

    nb = neighbours_ref[...]
    present = nb >= 0
    owner = nb // lanes
    offset = nb % lanes
    face_id = lax.broadcasted_iota(jnp.int32, nb.shape, 0)
    hop_of = jnp.where(face_id % 2 == 0, me - owner, owner - me)
    hop_of = jnp.where(present, hop_of, -1)
    far_count = counts_ref[jnp.maximum(me - HOPS, 0)]
    skipped = jnp.where((face_id % 2 == 0) & (hop_of == HOPS), far_count - half, 0)
    where_at = jnp.clip(offset - skipped, 0, lanes - 1)
    low_half = jnp.broadcast_to(lane < half, (8, lanes))
    tail_index = jnp.broadcast_to(own_count - half + lane % half, (8, lanes))
    head_index = jnp.broadcast_to(lane % half, (8, lanes))

    def pick(block, index):
        rows = block.shape[0]
        return jnp.concatenate(
            [
                jnp.take_along_axis(block[r : r + 8], index, axis=1, mode="promise_in_bounds")
                for r in range(0, rows, 8)
            ],
            axis=0,
        )

    def copy(stage, direction, hop, src, dst):
        sign = 1 if direction == 0 else -1
        target = (me + sign * hop + total) % total
        return pltpu.make_async_remote_copy(
            src_ref=src,
            dst_ref=dst,
            send_sem=send_sems.at[stage, direction, hop - 1],
            recv_sem=recv_sems.at[stage, direction, hop - 1],
            device_id=place(target),
            device_id_type=MESH,
        )

    finishing = []

    def exchange(stage, values, extent, faces, packed, near, far):
        area = extent * extent
        last = extent - 1
        for direction in (0, 1):
            at = last if direction == 0 else 0
            faces[direction, 0:area, :] = values[pl.ds(at * area, area), :]
            for x in range(extent):
                faces[direction, pl.ds(area + x * extent, extent), :] = values[
                    pl.ds(x * area + at * extent, extent), :
                ]
            faces[direction, pl.ds(2 * area, area), :] = values[pl.ds(at, area, extent), :]
            pack = 3 * area // 2
            index = tail_index if direction == 0 else head_index
            for r in range(0, pack, 8):
                a = jnp.take_along_axis(
                    faces[direction, pl.ds(r, 8), :], index, axis=1, mode="promise_in_bounds"
                )
                b = jnp.take_along_axis(
                    faces[direction, pl.ds(pack + r, 8), :], index, axis=1, mode="promise_in_bounds"
                )
                packed[direction, pl.ds(r, 8), :] = jnp.where(low_half, a, b)
        if stage == 0:
            pl.semaphore_wait(barrier, greeted)
        copies = []
        for hop in range(1, HOPS + 1):
            for direction in (0, 1):
                if hop < HOPS:
                    made = copy(stage, direction, hop, faces.at[direction], near.at[direction, hop - 1])
                else:
                    made = copy(stage, direction, hop, packed.at[direction], far.at[direction])
                sends = me + hop < total if direction == 0 else me >= hop
                takes = me >= hop if direction == 0 else me + hop < total
                pl.when(sends)(made.start)
                copies.append((made, takes))
                finishing.append((made, sends))
        for made, takes in copies:
            pl.when(takes)(made.wait_recv)
        ghosts = []
        pack = 3 * area // 2
        for face in range(6):
            direction, slot = face % 2, face // 2
            at = jnp.broadcast_to(where_at[face : face + 1, :], (8, lanes))
            at_high = jnp.minimum(at + half, lanes - 1)
            hops = jnp.broadcast_to(hop_of[face : face + 1, :], (8, lanes))
            pieces = []
            for r in range(0, area, 8):
                row = slot * area + r
                block = jnp.zeros((8, lanes), F32)
                for hop in range(HOPS + 1):
                    index = at
                    if hop == 0:
                        window = faces[direction, pl.ds(row, 8), :]
                    elif hop < HOPS:
                        window = near[direction, hop - 1, pl.ds(row, 8), :]
                    elif row < pack:
                        window = far[direction, pl.ds(row, 8), :]
                    else:
                        window = far[direction, pl.ds(row - pack, 8), :]
                        index = at_high
                    taken = jnp.take_along_axis(window, index, axis=1, mode="promise_in_bounds")
                    block = jnp.where(hops == hop, taken, block)
                pieces.append(block)
            ghosts.append(jnp.concatenate(pieces, axis=0))
        return ghosts

    zrow = lax.broadcasted_iota(jnp.int32, (8, 8, lanes), 1)

    def fine(values, ghosts, use):
        g0, g1, g2, g3, g4, g5 = ghosts
        zghost[pl.ds(0, 64, 8), :] = g4
        zghost[pl.ds(7, 64, 8), :] = g5
        for x in range(8):
            rows = pl.ds(64 * x, 64)
            here = values[rows, :]
            beside = (g0 if x == 0 else values[pl.ds(64 * (x - 1), 64), :]) + (
                g1 if x == 7 else values[pl.ds(64 * (x + 1), 64), :]
            )
            beside = beside + jnp.concatenate([g2[8 * x : 8 * x + 8], here[:-8]], axis=0)
            beside = beside + jnp.concatenate([here[8:], g3[8 * x : 8 * x + 8]], axis=0)
            cube = here.reshape(8, 8, lanes)
            edge = zghost[rows, :].reshape(8, 8, lanes)
            below = jnp.where(zrow == 0, edge, pltpu.roll(cube, 1, 1))
            above = jnp.where(zrow == 7, edge, pltpu.roll(cube, 7, 1))
            beside = beside + (below + above).reshape(64, lanes)
            use(x, rows, here, 6.0 * here - beside)

    def exchange_fine(stage, values):
        return exchange(
            stage,
            values,
            8,
            faces_fine.at[stage],
            packed_fine.at[stage],
            near_fine.at[stage],
            far_fine.at[stage],
        )

    def sweep(x, rows, here, applied):
        second[rows, :] = here + RELAX_FINE * (source[rows, :] - applied)

    fine(first, exchange_fine(0, first), sweep)

    slabs = []

    def restrict(x, rows, here, applied):
        slabs.append(source[rows, :] - applied)
        if x % 2 == 1:
            both = slabs[x - 1] + slabs[x]
            for y in range(4):
                paired[pl.ds(32 * (x // 2) + 8 * y, 8), :] = (
                    both[16 * y : 16 * y + 8] + both[16 * y + 8 : 16 * y + 16]
                )

    fine(second, exchange_fine(1, second), restrict)
    coarse_rhs = 0.125 * (paired[pl.ds(0, 64, 2), :] + paired[pl.ds(1, 64, 2), :])
    coarse_one = RELAX_COARSE * coarse_rhs
    coarse[...] = coarse_one
    g0, g1, g2, g3, g4, g5 = exchange(
        4, coarse, 4, faces_coarse, packed_coarse, near_coarse, far_coarse
    )
    beside = jnp.concatenate([g0, coarse_one[:-16]], axis=0) + jnp.concatenate(
        [coarse_one[16:], g1], axis=0
    )
    for k, shift in enumerate((4, 60, 1, 63)):
        shifted[k, :, :] = pltpu.roll(coarse_one, shift, 0)
    for x in range(4):
        shifted[0, pl.ds(16 * x, 4), :] = g2[4 * x : 4 * x + 4]
        shifted[1, pl.ds(16 * x + 12, 4), :] = g3[4 * x : 4 * x + 4]
    for x in range(4):
        for y in range(4):
            at = 16 * x + 4 * y
            shifted[2, pl.ds(at, 1), :] = g4[4 * x + y : 4 * x + y + 1]
            shifted[3, pl.ds(at + 3, 1), :] = g5[4 * x + y : 4 * x + y + 1]
    beside = beside + (shifted[0] + shifted[1]) + (shifted[2] + shifted[3])
    coarse_two = coarse_one + RELAX_COARSE * (coarse_rhs - 0.25 * (6.0 * coarse_one - beside))
    paired[pl.ds(0, 64, 2), :] = coarse_two
    paired[pl.ds(1, 64, 2), :] = coarse_two
    for x in range(8):
        for y in range(8):
            rows = pl.ds(64 * x + 8 * y, 8)
            second[rows, :] = second[rows, :] + paired[pl.ds(32 * (x // 2) + 8 * (y // 2), 8), :]

    def smooth(x, rows, here, applied):
        first[rows, :] = here + RELAX_FINE * (source[rows, :] - applied)

    fine(second, exchange_fine(2, second), smooth)

    parts = [jnp.zeros((8, lanes), F32)] * 5

    def fold(block):
        return jnp.sum(block.reshape(8, 8, lanes), axis=0)

    def finish(x, rows, here, applied):
        image[rows, :] = applied
        r = source[rows, :]
        for k, term in enumerate((r * here, here * applied, r * r, r * applied, applied * applied)):
            parts[k] = parts[k] + fold(term)

    fine(first, exchange_fine(3, first), finish)

    row = lax.broadcasted_iota(jnp.int32, (8, lanes), 0)
    tile = jnp.zeros((8, lanes), F32)
    for k in range(5):
        tile = jnp.where(row == k, jnp.sum(parts[k], axis=0, keepdims=True), tile)
    base = 0
    for size, mine, partner in stages:
        sums[base + mine] = tile
        copies = []
        for k in range(1, size):
            made = pltpu.make_async_remote_copy(
                src_ref=sums.at[base + mine],
                dst_ref=sums.at[base + mine],
                send_sem=sum_send.at[base + k],
                recv_sem=sum_recv.at[base + k],
                device_id=partner(k),
                device_id_type=MESH,
            )
            made.start()
            copies.append(made)
        for made in copies:
            made.wait_recv()
        tile = jnp.sum(sums[base : base + size], axis=0)
        for made in copies:
            made.wait_send()
        base += size
    whole = jnp.sum(tile, axis=1, keepdims=True)
    along, curvature, old_square, cross, image_square = [whole[k : k + 1] for k in range(5)]
    step = along / curvature
    square = old_square - 2.0 * step * cross + step * step * image_square
    norm_ref[...] = jnp.broadcast_to(jnp.sqrt(square), norm_ref.shape)
    for x in range(8):
        rows = pl.ds(64 * x, 64)
        solution_ref[rows, :] = step * first[rows, :]
        residual_ref[rows, :] = source[rows, :] - step * image[rows, :]
    for made, sends in finishing:
        pl.when(sends)(made.wait_send)


def local(sizes, right_side, counts, neighbours):
    cells, lanes = right_side.shape
    curve_size, level_size = sizes
    total = curve_size * level_size

    def body(*refs):
        curve, level = lax.axis_index("curve"), lax.axis_index("level")
        if total <= 64:
            me = curve * level_size + level

            def everyone(k):
                other = (me + k) % total
                return (other // level_size, other % level_size)

            stages = [(total, me, everyone)]
        else:
            stages = [
                (level_size, level, lambda k: (curve, (level + k) % level_size)),
                (curve_size, curve, lambda k: ((curve + k) % curve_size, level)),
            ]
        kernel(sizes, stages, *refs)

    sum_rows = total if total <= 64 else curve_size + level_size
    vmem = pl.BlockSpec(memory_space=pltpu.VMEM)
    block = jax.ShapeDtypeStruct((cells, lanes), F32)
    out = pl.pallas_call(
        body,
        out_shape=(block, block, jax.ShapeDtypeStruct((8, lanes), F32)),
        in_specs=[vmem, pl.BlockSpec(memory_space=pltpu.SMEM), vmem],
        out_specs=(vmem, vmem, vmem),
        scratch_shapes=[
            pltpu.VMEM((cells, lanes), F32),
            pltpu.VMEM((cells, lanes), F32),
            pltpu.VMEM((cells, lanes), F32),
            pltpu.VMEM((cells, lanes), F32),
            pltpu.VMEM((cells, lanes), F32),
            pltpu.VMEM((cells // 4, lanes), F32),
            pltpu.VMEM((cells // 8, lanes), F32),
            pltpu.VMEM((4, cells // 8, lanes), F32),
            pltpu.VMEM((4, 2, 192, lanes), F32),
            pltpu.VMEM((4, 2, 96, lanes), F32),
            pltpu.VMEM((4, 2, 2, 192, lanes), F32),
            pltpu.VMEM((4, 2, 96, lanes), F32),
            pltpu.VMEM((2, 48, lanes), F32),
            pltpu.VMEM((2, 24, lanes), F32),
            pltpu.VMEM((2, 2, 48, lanes), F32),
            pltpu.VMEM((2, 24, lanes), F32),
            pltpu.VMEM((sum_rows, 8, lanes), F32),
            pltpu.SemaphoreType.DMA((5, 2, HOPS)),
            pltpu.SemaphoreType.DMA((5, 2, HOPS)),
            pltpu.SemaphoreType.DMA((sum_rows,)),
            pltpu.SemaphoreType.DMA((sum_rows,)),
        ],
        compiler_params=pltpu.CompilerParams(collective_id=0, has_side_effects=True),
    )(right_side, counts, neighbours)
    return out[0], out[1], out[2][0, 0]


def solution(mesh):
    sizes = tuple(mesh.shape[name] for name in AXES)
    in_specs = (P(None, AXES), P(), P(None, AXES))
    out_specs = (P(None, AXES), P(None, AXES), P())
    return jax.shard_map(
        functools.partial(local, sizes), mesh=mesh, in_specs=in_specs, out_specs=out_specs, check_vma=False
    )
```

time: 250 us -> 59 us (0.24)
  starting transfers between devices: 83.7 us -> 0 us
  local copies, waits for them, and re-layouts: 76.8 us -> 3.61 us
  Pallas kernels: 0 us -> 54.6 us
  blocking collectives: 43.2 us -> 0 us
  waiting for transfers between devices: 24.4 us -> 0 us
  other arithmetic: 11.1 us -> 0 us
  between operations: 8.26 us -> 0.64 us
    ppermute x30 -> x0, starting transfers between devices: 83.7 us -> none  [from_behind(): return lax.ppermute(block, axis, route)]
    pallas_call x0 -> x1, Pallas kernels: none -> 54.6 us  [local(): pl.pallas_call(body, out_shape=(block, block, jax.ShapeDtypeStruct((8, la...]
    psum x1 -> x0, blocking collectives: 43.2 us -> none  [local(): lax.psum((local_along, local_curvature, jnp.sum(residual_in * residual_in...]
    gather x33 -> x0, local copies, waits for them, and re-layouts: 37.8 us -> none  [the longest x30 23.5 us: exchange(): picked = jnp.take(lookup, position[face_id], axis=1)]
    ppermute x30 -> x0, waiting for transfers between devices: 24.4 us -> none  [from_behind(): return lax.ppermute(block, axis, route)]
    unnamed x148 -> x4, local copies, waits for them, and re-layouts: 20.8 us -> 2.42 us
    squeeze x30 -> x0, local copies, waits for them, and re-layouts: 4.09 us -> none  [exchange(): window[face_id // 2]]
    scatter x30 -> x0, local copies, waits for them, and re-layouts: 4.06 us -> none  [the longest x5 0.7 us: apply_operator(): padded = padded.at[1:-1, 0, 1:-1].set(shaped[2])]
  transfers between devices with their start and end apart: 30 -> 0, of which waited for: 5 -> 0; matrix products, arithmetic and copies ran while one was open for 17% -> 0% of each run, Pallas kernels for 0% -> 0%
where the time goes in v1:
time: 59 us; the launch traced here: 58.8 us
  Pallas kernels  54.6 us (93%)
  local copies, waits for them, and re-layouts  3.61 us (6%)
  between operations  0.64 us (1%)
    pallas_call x1, Pallas kernels, local(): pl.pallas_call(body, out_shape=(block, block, jax.ShapeDtypeStruct((8, la...  54.6 us
    unnamed x4, local copies, waits for them, and re-layouts  2.42 us
    slice x1, local copies, waits for them, and re-layouts, local(): return (out[0], out[1], out[2][0, 0])  1.19 us

profile of v1, /device:TPU:0, one launch (start us, length us, event | category | flops | bytes accessed | tf_op | source)
XLA Modules:
  0.0 58.8 jit_solution(7684992423799221579)
XLA Ops:
  0.6 54.6 %shard_map.58 = (f32[512,128]{1,0:T(8,128)}, f32[512,128]{1,0:T(8,128)}, f32[8,128]{1,0:T(8,128)}) custom-call(f32[512,128]{1,0:T(8,128)} %refs_0_.1, s32[32]{0:T(128)} %refs_1_.1, s32[6,128]{1,0:T(8,128)} %refs_2_.1), custom_call_target="tpu_custom_call" | custom-call | tf_op jit(solution)/shard_map/pallas_call | solution.py:345
  55.2 1.2 %slice.3 = f32[1,1]{1,0:T(1,128)} slice(f32[8,128]{1,0:T(8,128)} %get-tuple-element.8), slice={[0:1], [0:1]} | slice | bytes 8 | tf_op jit(solution)/shard_map/slice | solution.py:375
  56.4 0.0 copy-start
  56.4 1.7 %copy.8 = f32[512,128]{1,0:T(8,128)} copy(f32[512,128]{1,0:T(8,128)} %get-tuple-element.12) | data formatting | bytes 524288
  58.1 0.0 copy-done
  58.1 0.7 %copy.9 = f32[512,128]{1,0:T(8,128)} copy(f32[512,128]{1,0:T(8,128)S(1)} %copy-done) | data formatting | bytes 524288
Async XLA Ops:
  56.4 1.7 %copy-start = (f32[512,128]{1,0:T(8,128)S(1)}, f32[512,128]{1,0:T(8,128)}, u32[]{:S(2)}) copy-start(f32[512,128]{1,0:T(8,128)} %get-tuple-element.13) | copy-start | bytes 786436

commit v2 on v1

--- a/solution.py
+++ b/solution.py
@@ -35,6 +35,7 @@
     paired,
     coarse,
     shifted,
+    doubled,
     faces_fine,
     packed_fine,
     near_fine,
@@ -205,21 +206,26 @@
             beside = beside + (below + above).reshape(64, lanes)
             use(x, rows, here, 6.0 * here - beside)
 
-    def exchange_fine(stage, values):
+    def exchange_fine(stage, k, values):
+        return exchange(
+            stage, values, 8, faces_fine.at[k], packed_fine.at[k], near_fine.at[k], far_fine.at[k]
+        )
+
+    def exchange_coarse(stage, k):
         return exchange(
             stage,
-            values,
-            8,
-            faces_fine.at[stage],
-            packed_fine.at[stage],
-            near_fine.at[stage],
-            far_fine.at[stage],
+            coarse,
+            4,
+            faces_coarse.at[k],
+            packed_coarse.at[k],
+            near_coarse.at[k],
+            far_coarse.at[k],
         )
 
     def sweep(x, rows, here, applied):
         second[rows, :] = here + RELAX_FINE * (source[rows, :] - applied)
 
-    fine(first, exchange_fine(0, first), sweep)
+    fine(first, exchange_fine(0, 0, first), sweep)
 
     slabs = []
 
@@ -232,13 +238,12 @@
                     both[16 * y : 16 * y + 8] + both[16 * y + 8 : 16 * y + 16]
                 )
 
-    fine(second, exchange_fine(1, second), restrict)
+    ghosts = exchange_fine(1, 1, second)
+    fine(second, ghosts, restrict)
     coarse_rhs = 0.125 * (paired[pl.ds(0, 64, 2), :] + paired[pl.ds(1, 64, 2), :])
     coarse_one = RELAX_COARSE * coarse_rhs
     coarse[...] = coarse_one
-    g0, g1, g2, g3, g4, g5 = exchange(
-        4, coarse, 4, faces_coarse, packed_coarse, near_coarse, far_coarse
-    )
+    g0, g1, g2, g3, g4, g5 = exchange_coarse(2, 0)
     beside = jnp.concatenate([g0, coarse_one[:-16]], axis=0) + jnp.concatenate(
         [coarse_one[16:], g1], axis=0
     )
@@ -254,6 +259,7 @@
             shifted[3, pl.ds(at + 3, 1), :] = g5[4 * x + y : 4 * x + y + 1]
     beside = beside + (shifted[0] + shifted[1]) + (shifted[2] + shifted[3])
     coarse_two = coarse_one + RELAX_COARSE * (coarse_rhs - 0.25 * (6.0 * coarse_one - beside))
+    coarse[...] = coarse_two
     paired[pl.ds(0, 64, 2), :] = coarse_two
     paired[pl.ds(1, 64, 2), :] = coarse_two
     for x in range(8):
@@ -261,10 +267,18 @@
             rows = pl.ds(64 * x + 8 * y, 8)
             second[rows, :] = second[rows, :] + paired[pl.ds(32 * (x // 2) + 8 * (y // 2), 8), :]
 
+    corrections = exchange_coarse(3, 1)
+    for face in range(6):
+        doubled[face, pl.ds(0, 16, 2), :] = corrections[face]
+        doubled[face, pl.ds(1, 16, 2), :] = corrections[face]
+        ghosts[face] = ghosts[face] + jnp.concatenate(
+            [doubled[face, pl.ds(8 * (a // 2), 8), :] for a in range(8)], axis=0
+        )
+
     def smooth(x, rows, here, applied):
         first[rows, :] = here + RELAX_FINE * (source[rows, :] - applied)
 
-    fine(second, exchange_fine(2, second), smooth)
+    fine(second, ghosts, smooth)
 
     parts = [jnp.zeros((8, lanes), F32)] * 5
 
@@ -277,7 +291,7 @@
         for k, term in enumerate((r * here, here * applied, r * r, r * applied, applied * applied)):
             parts[k] = parts[k] + fold(term)
 
-    fine(first, exchange_fine(3, first), finish)
+    fine(first, exchange_fine(4, 2, first), finish)
 
     row = lax.broadcasted_iota(jnp.int32, (8, lanes), 0)
     tile = jnp.zeros((8, lanes), F32)
@@ -356,14 +370,15 @@
             pltpu.VMEM((cells // 4, lanes), F32),
             pltpu.VMEM((cells // 8, lanes), F32),
             pltpu.VMEM((4, cells // 8, lanes), F32),
-            pltpu.VMEM((4, 2, 192, lanes), F32),
-            pltpu.VMEM((4, 2, 96, lanes), F32),
-            pltpu.VMEM((4, 2, 2, 192, lanes), F32),
-            pltpu.VMEM((4, 2, 96, lanes), F32),
-            pltpu.VMEM((2, 48, lanes), F32),
-            pltpu.VMEM((2, 24, lanes), F32),
+            pltpu.VMEM((6, 32, lanes), F32),
+            pltpu.VMEM((3, 2, 192, lanes), F32),
+            pltpu.VMEM((3, 2, 96, lanes), F32),
+            pltpu.VMEM((3, 2, 2, 192, lanes), F32),
+            pltpu.VMEM((3, 2, 96, lanes), F32),
             pltpu.VMEM((2, 2, 48, lanes), F32),
-            pltpu.VMEM((2, 24, lanes), F32),
+            pltpu.VMEM((2, 2, 24, lanes), F32),
+            pltpu.VMEM((2, 2, 2, 48, lanes), F32),
+            pltpu.VMEM((2, 2, 24, lanes), F32),
             pltpu.VMEM((sum_rows, 8, lanes), F32),
             pltpu.SemaphoreType.DMA((5, 2, HOPS)),
             pltpu.SemaphoreType.DMA((5, 2, HOPS)),

time: 59 us -> 54.6 us (0.925)
  Pallas kernels: 54.6 us -> 50.2 us
    pallas_call x1, Pallas kernels: 54.6 us -> 50.2 us  [local(): pl.pallas_call(body, out_shape=(block, block, jax.ShapeDtypeStruct((8, la...]
where the time goes in v2:
time: 54.6 us; the launch traced here: 54.4 us
  Pallas kernels  50.2 us (92%)
  local copies, waits for them, and re-layouts  3.61 us (7%)
  between operations  0.64 us (1%)
    pallas_call x1, Pallas kernels, local(): pl.pallas_call(body, out_shape=(block, block, jax.ShapeDtypeStruct((8, la...  50.2 us
    unnamed x4, local copies, waits for them, and re-layouts  2.42 us
    slice x1, local copies, waits for them, and re-layouts, local(): return (out[0], out[1], out[2][0, 0])  1.19 us

profile of v2, /device:TPU:0, one launch (start us, length us, event | category | flops | bytes accessed | tf_op | source)
XLA Modules:
  0.0 54.4 jit_solution(9224273772626923270)
XLA Ops:
  0.6 50.2 %shard_map.58 = (f32[512,128]{1,0:T(8,128)}, f32[512,128]{1,0:T(8,128)}, f32[8,128]{1,0:T(8,128)}) custom-call(f32[512,128]{1,0:T(8,128)} %refs_0_.1, s32[32]{0:T(128)} %refs_1_.1, s32[6,128]{1,0:T(8,128)} %refs_2_.1), custom_call_target="tpu_custom_call" | custom-call | tf_op jit(solution)/shard_map/pallas_call | solution.py:359
  50.8 1.2 %slice.3 = f32[1,1]{1,0:T(1,128)} slice(f32[8,128]{1,0:T(8,128)} %get-tuple-element.8), slice={[0:1], [0:1]} | slice | bytes 8 | tf_op jit(solution)/shard_map/slice | solution.py:390
  52.0 0.0 copy-start
  52.0 1.7 %copy.8 = f32[512,128]{1,0:T(8,128)} copy(f32[512,128]{1,0:T(8,128)} %get-tuple-element.12) | data formatting | bytes 524288
  53.7 0.0 copy-done
  53.7 0.7 %copy.9 = f32[512,128]{1,0:T(8,128)} copy(f32[512,128]{1,0:T(8,128)S(1)} %copy-done) | data formatting | bytes 524288
Async XLA Ops:
  52.0 1.7 %copy-start = (f32[512,128]{1,0:T(8,128)S(1)}, f32[512,128]{1,0:T(8,128)}, u32[]{:S(2)}) copy-start(f32[512,128]{1,0:T(8,128)} %get-tuple-element.13) | copy-start | bytes 786436

commit v3 on v2

--- a/solution.py
+++ b/solution.py
@@ -38,18 +38,16 @@
     doubled,
     faces_fine,
     packed_fine,
-    near_fine,
-    far_fine,
+    windows_fine,
     faces_coarse,
     packed_coarse,
-    near_coarse,
-    far_coarse,
+    windows_coarse,
     sums,
-    send_sems,
-    recv_sems,
-    sum_send,
-    sum_recv,
+    *sems,
 ):
+    link_sems, relay_sems, pair_sems, far_sems, (sum_send, sum_recv) = [
+        sems[i : i + 2] for i in range(0, 10, 2)
+    ]
     curve_size, level_size = sizes
     total = curve_size * level_size
     me = lax.axis_index("curve") * level_size + lax.axis_index("level")
@@ -61,9 +59,9 @@
 
     barrier = pltpu.get_barrier_semaphore()
     greeted = 0
-    for size, _, partner in stages:
+    for size, _, peer in stages:
         for k in range(1, size):
-            pl.semaphore_signal(barrier, inc=1, device_id=partner(k), device_id_type=MESH)
+            pl.semaphore_signal(barrier, inc=1, device_id=peer(k), device_id_type=MESH)
             greeted += 1
     direct = len(stages) == 1
     if not direct:
@@ -90,39 +88,43 @@
     hop_of = jnp.where(face_id % 2 == 0, me - owner, owner - me)
     hop_of = jnp.where(present, hop_of, -1)
     far_count = counts_ref[jnp.maximum(me - HOPS, 0)]
-    skipped = jnp.where((face_id % 2 == 0) & (hop_of == HOPS), far_count - half, 0)
+    odd = me % 2
+    even = 1 - odd
+    partner = me + 1 - 2 * odd
+    earlier_pair = me >= 2
+    later_pair = me - odd + 2 < total
+    reaches = (1 + 2 * even, 1 + 2 * odd)
+    arrives = (2 * odd, 2 * even)
+    far_there = jnp.where(odd == 1, me + HOPS < total, me >= HOPS)
+    far_device = (me + HOPS * (2 * odd - 1) + total) % total
+    skipped = jnp.where(
+        (face_id % 2 == 0) & (hop_of == HOPS), even * (far_count - half), 0
+    )
     where_at = jnp.clip(offset - skipped, 0, lanes - 1)
     low_half = jnp.broadcast_to(lane < half, (8, lanes))
-    tail_index = jnp.broadcast_to(own_count - half + lane % half, (8, lanes))
-    head_index = jnp.broadcast_to(lane % half, (8, lanes))
+    pack_index = jnp.broadcast_to(odd * (own_count - half) + lane % half, (8, lanes))
 
     def pick(block, index):
-        rows = block.shape[0]
-        return jnp.concatenate(
-            [
-                jnp.take_along_axis(block[r : r + 8], index, axis=1, mode="promise_in_bounds")
-                for r in range(0, rows, 8)
-            ],
-            axis=0,
-        )
-
-    def copy(stage, direction, hop, src, dst):
-        sign = 1 if direction == 0 else -1
-        target = (me + sign * hop + total) % total
-        return pltpu.make_async_remote_copy(
+        return jnp.take_along_axis(block, index, axis=1, mode="promise_in_bounds")
+
+    finishing = []
+
+    def send(src, dst, sems, at, target, sends):
+        made = pltpu.make_async_remote_copy(
             src_ref=src,
             dst_ref=dst,
-            send_sem=send_sems.at[stage, direction, hop - 1],
-            recv_sem=recv_sems.at[stage, direction, hop - 1],
+            send_sem=sems[0].at[at],
+            recv_sem=sems[1].at[at],
             device_id=place(target),
             device_id_type=MESH,
         )
-
-    finishing = []
-
-    def exchange(stage, values, extent, faces, packed, near, far):
+        finishing.append((made, sends))
+        return made
+
+    def exchange(stage, values, extent, faces, packed, windows):
         area = extent * extent
         last = extent - 1
+        pack = 3 * area // 2
         for direction in (0, 1):
             at = last if direction == 0 else 0
             faces[direction, 0:area, :] = values[pl.ds(at * area, area), :]
@@ -131,38 +133,62 @@
                     pl.ds(x * area + at * extent, extent), :
                 ]
             faces[direction, pl.ds(2 * area, area), :] = values[pl.ds(at, area, extent), :]
-            pack = 3 * area // 2
-            index = tail_index if direction == 0 else head_index
-            for r in range(0, pack, 8):
-                a = jnp.take_along_axis(
-                    faces[direction, pl.ds(r, 8), :], index, axis=1, mode="promise_in_bounds"
-                )
-                b = jnp.take_along_axis(
-                    faces[direction, pl.ds(pack + r, 8), :], index, axis=1, mode="promise_in_bounds"
-                )
-                packed[direction, pl.ds(r, 8), :] = jnp.where(low_half, a, b)
         if stage == 0:
             pl.semaphore_wait(barrier, greeted)
-        copies = []
-        for hop in range(1, HOPS + 1):
+        links = []
+        for chunk in range(3):
+            rows = pl.ds(chunk * area, area)
             for direction in (0, 1):
-                if hop < HOPS:
-                    made = copy(stage, direction, hop, faces.at[direction], near.at[direction, hop - 1])
-                else:
-                    made = copy(stage, direction, hop, packed.at[direction], far.at[direction])
-                sends = me + hop < total if direction == 0 else me >= hop
-                takes = me >= hop if direction == 0 else me + hop < total
-                pl.when(sends)(made.start)
-                copies.append((made, takes))
-                finishing.append((made, sends))
-        for made, takes in copies:
-            pl.when(takes)(made.wait_recv)
+                reach = reaches[direction]
+                target = me + reach if direction == 0 else me - reach
+                made = send(
+                    faces.at[direction, rows],
+                    windows.at[direction, reach - 1, rows],
+                    link_sems,
+                    (stage, direction, chunk),
+                    (target + total) % total,
+                    later_pair if direction == 0 else earlier_pair,
+                )
+                pl.when(later_pair if direction == 0 else earlier_pair)(made.start)
+                links.append((direction, chunk, rows, made))
+        inside = send(faces.at[odd], windows.at[odd, 0], pair_sems, (stage,), partner, None)
+        inside.start()
+        for r in range(0, pack, 8):
+            a = pick(faces[1 - odd, pl.ds(r, 8), :], pack_index)
+            b = pick(faces[1 - odd, pl.ds(pack + r, 8), :], pack_index)
+            packed[pl.ds(r, 8), :] = jnp.where(low_half, a, b)
+        far = send(
+            packed, windows.at[1 - odd, 2, pl.ds(0, pack)], far_sems, (stage,), far_device, far_there
+        )
+        pl.when(far_there)(far.start)
+        relays = []
+        for direction, chunk, rows, made in links:
+            comes = earlier_pair if direction == 0 else later_pair
+            relay = send(
+                windows.at[direction, arrives[direction], rows],
+                windows.at[direction, 1, rows],
+                relay_sems,
+                (stage, direction, chunk),
+                partner,
+                comes,
+            )
+
+            @pl.when(comes)
+            def _():
+                made.wait_recv()
+                relay.start()
+
+            relays.append((relay, comes))
+        inside.wait_recv()
+        pl.when(far_there)(far.wait_recv)
+        for relay, comes in relays:
+            pl.when(comes)(relay.wait_recv)
         ghosts = []
-        pack = 3 * area // 2
         for face in range(6):
             direction, slot = face % 2, face // 2
             at = jnp.broadcast_to(where_at[face : face + 1, :], (8, lanes))
-            at_high = jnp.minimum(at + half, lanes - 1)
+            is_packed = odd == direction
+            at_high = jnp.where(is_packed, jnp.minimum(at + half, lanes - 1), at)
             hops = jnp.broadcast_to(hop_of[face : face + 1, :], (8, lanes))
             pieces = []
             for r in range(0, area, 8):
@@ -172,15 +198,13 @@
                     index = at
                     if hop == 0:
                         window = faces[direction, pl.ds(row, 8), :]
-                    elif hop < HOPS:
-                        window = near[direction, hop - 1, pl.ds(row, 8), :]
-                    elif row < pack:
-                        window = far[direction, pl.ds(row, 8), :]
+                    elif hop < HOPS or row < pack:
+                        window = windows[direction, hop - 1, pl.ds(row, 8), :]
                     else:
-                        window = far[direction, pl.ds(row - pack, 8), :]
+                        start = pl.multiple_of(row - jnp.where(is_packed, pack, 0), 8)
+                        window = windows[direction, hop - 1, pl.ds(start, 8), :]
                         index = at_high
-                    taken = jnp.take_along_axis(window, index, axis=1, mode="promise_in_bounds")
-                    block = jnp.where(hops == hop, taken, block)
+                    block = jnp.where(hops == hop, pick(window, index), block)
                 pieces.append(block)
             ghosts.append(jnp.concatenate(pieces, axis=0))
         return ghosts
@@ -208,18 +232,12 @@
 
     def exchange_fine(stage, k, values):
         return exchange(
-            stage, values, 8, faces_fine.at[k], packed_fine.at[k], near_fine.at[k], far_fine.at[k]
+            stage, values, 8, faces_fine.at[k], packed_fine.at[k], windows_fine.at[k]
         )
 
     def exchange_coarse(stage, k):
         return exchange(
-            stage,
-            coarse,
-            4,
-            faces_coarse.at[k],
-            packed_coarse.at[k],
-            near_coarse.at[k],
-            far_coarse.at[k],
+            stage, coarse, 4, faces_coarse.at[k], packed_coarse.at[k], windows_coarse.at[k]
         )
 
     def sweep(x, rows, here, applied):
@@ -298,7 +316,7 @@
     for k in range(5):
         tile = jnp.where(row == k, jnp.sum(parts[k], axis=0, keepdims=True), tile)
     base = 0
-    for size, mine, partner in stages:
+    for size, mine, peer in stages:
         sums[base + mine] = tile
         copies = []
         for k in range(1, size):
@@ -307,7 +325,7 @@
                 dst_ref=sums.at[base + mine],
                 send_sem=sum_send.at[base + k],
                 recv_sem=sum_recv.at[base + k],
-                device_id=partner(k),
+                device_id=peer(k),
                 device_id_type=MESH,
             )
             made.start()
@@ -328,7 +346,10 @@
         solution_ref[rows, :] = step * first[rows, :]
         residual_ref[rows, :] = source[rows, :] - step * image[rows, :]
     for made, sends in finishing:
-        pl.when(sends)(made.wait_send)
+        if sends is None:
+            made.wait_send()
+        else:
+            pl.when(sends)(made.wait_send)
 
 
 def local(sizes, right_side, counts, neighbours):
@@ -372,16 +393,20 @@
             pltpu.VMEM((4, cells // 8, lanes), F32),
             pltpu.VMEM((6, 32, lanes), F32),
             pltpu.VMEM((3, 2, 192, lanes), F32),
-            pltpu.VMEM((3, 2, 96, lanes), F32),
-            pltpu.VMEM((3, 2, 2, 192, lanes), F32),
-            pltpu.VMEM((3, 2, 96, lanes), F32),
+            pltpu.VMEM((3, 96, lanes), F32),
+            pltpu.VMEM((3, 2, HOPS, 192, lanes), F32),
             pltpu.VMEM((2, 2, 48, lanes), F32),
-            pltpu.VMEM((2, 2, 24, lanes), F32),
-            pltpu.VMEM((2, 2, 2, 48, lanes), F32),
-            pltpu.VMEM((2, 2, 24, lanes), F32),
+            pltpu.VMEM((2, 24, lanes), F32),
+            pltpu.VMEM((2, 2, HOPS, 48, lanes), F32),
             pltpu.VMEM((sum_rows, 8, lanes), F32),
-            pltpu.SemaphoreType.DMA((5, 2, HOPS)),
-            pltpu.SemaphoreType.DMA((5, 2, HOPS)),
+            pltpu.SemaphoreType.DMA((5, 2, 3)),
+            pltpu.SemaphoreType.DMA((5, 2, 3)),
+            pltpu.SemaphoreType.DMA((5, 2, 3)),
+            pltpu.SemaphoreType.DMA((5, 2, 3)),
+            pltpu.SemaphoreType.DMA((5,)),
+            pltpu.SemaphoreType.DMA((5,)),
+            pltpu.SemaphoreType.DMA((5,)),
+            pltpu.SemaphoreType.DMA((5,)),
             pltpu.SemaphoreType.DMA((sum_rows,)),
             pltpu.SemaphoreType.DMA((sum_rows,)),
         ],

time: 54.6 us -> 50 us (0.916)
  Pallas kernels: 50.2 us -> 45.6 us
    pallas_call x1, Pallas kernels: 50.2 us -> 45.6 us  [local(): pl.pallas_call(body, out_shape=(block, block, jax.ShapeDtypeStruct((8, la...]
where the time goes in v3:
time: 50 us; the launch traced here: 49.8 us
  Pallas kernels  45.6 us (91%)
  local copies, waits for them, and re-layouts  3.61 us (7%)
  between operations  0.64 us (1%)
    pallas_call x1, Pallas kernels, local(): pl.pallas_call(body, out_shape=(block, block, jax.ShapeDtypeStruct((8, la...  45.6 us
    unnamed x4, local copies, waits for them, and re-layouts  2.42 us
    slice x1, local copies, waits for them, and re-layouts, local(): return (out[0], out[1], out[2][0, 0])  1.19 us

profile of v3, /device:TPU:0, one launch (start us, length us, event | category | flops | bytes accessed | tf_op | source)
XLA Modules:
  0.0 49.8 jit_solution(14974343162999602897)
XLA Ops:
  0.6 45.6 %shard_map.58 = (f32[512,128]{1,0:T(8,128)}, f32[512,128]{1,0:T(8,128)}, f32[8,128]{1,0:T(8,128)}) custom-call(f32[512,128]{1,0:T(8,128)} %refs_0_.1, s32[32]{0:T(128)} %refs_1_.1, s32[6,128]{1,0:T(8,128)} %refs_2_.1), custom_call_target="tpu_custom_call" | custom-call | tf_op jit(solution)/shard_map/pallas_call | solution.py:380
  46.2 1.2 %slice.3 = f32[1,1]{1,0:T(1,128)} slice(f32[8,128]{1,0:T(8,128)} %get-tuple-element.8), slice={[0:1], [0:1]} | slice | bytes 8 | tf_op jit(solution)/shard_map/slice | solution.py:415
  47.4 0.0 copy-start
  47.4 1.7 %copy.8 = f32[512,128]{1,0:T(8,128)} copy(f32[512,128]{1,0:T(8,128)} %get-tuple-element.12) | data formatting | bytes 524288
  49.1 0.0 copy-done
  49.1 0.7 %copy.9 = f32[512,128]{1,0:T(8,128)} copy(f32[512,128]{1,0:T(8,128)S(1)} %copy-done) | data formatting | bytes 524288
Async XLA Ops:
  47.4 1.7 %copy-start = (f32[512,128]{1,0:T(8,128)S(1)}, f32[512,128]{1,0:T(8,128)}, u32[]{:S(2)}) copy-start(f32[512,128]{1,0:T(8,128)} %get-tuple-element.13) | copy-start | bytes 786436

commit v4 on v3

--- a/solution.py
+++ b/solution.py
@@ -36,6 +36,8 @@
     coarse,
     shifted,
     doubled,
+    held,
+    applied_ref,
     faces_fine,
     packed_fine,
     windows_fine,
@@ -121,7 +123,7 @@
         finishing.append((made, sends))
         return made
 
-    def exchange(stage, values, extent, faces, packed, windows):
+    def exchange(stage, values, extent, faces, packed, windows, meanwhile):
         area = extent * extent
         last = extent - 1
         pack = 3 * area // 2
@@ -161,6 +163,35 @@
             packed, windows.at[1 - odd, 2, pl.ds(0, pack)], far_sems, (stage,), far_device, far_there
         )
         pl.when(far_there)(far.start)
+        def ghost(face, hops_in, blocks):
+            direction, slot = face % 2, face // 2
+            at = jnp.broadcast_to(where_at[face : face + 1, :], (8, lanes))
+            is_packed = odd == direction
+            at_high = jnp.where(is_packed, jnp.minimum(at + half, lanes - 1), at)
+            hops = jnp.broadcast_to(hop_of[face : face + 1, :], (8, lanes))
+            pieces = []
+            for r in range(0, area, 8):
+                row = slot * area + r
+                block = blocks[r // 8]
+                for hop in hops_in:
+                    index = at
+                    if hop == 0:
+                        window = faces[direction, pl.ds(row, 8), :]
+                    elif hop < HOPS or row < pack:
+                        window = windows[direction, hop - 1, pl.ds(row, 8), :]
+                    else:
+                        start = pl.multiple_of(row - jnp.where(is_packed, pack, 0), 8)
+                        window = windows[direction, hop - 1, pl.ds(start, 8), :]
+                        index = at_high
+                    block = jnp.where(hops == hop, pick(window, index), block)
+                pieces.append(block)
+            return pieces
+
+        empty = [jnp.zeros((8, lanes), F32)] * (area // 8)
+        for face in range(6):
+            for r, block in enumerate(ghost(face, (0,), empty)):
+                held[face, pl.ds(8 * r, 8), :] = block
+        meanwhile()
         relays = []
         for direction, chunk, rows, made in links:
             comes = earlier_pair if direction == 0 else later_pair
@@ -181,35 +212,35 @@
             relays.append((relay, comes))
         inside.wait_recv()
         pl.when(far_there)(far.wait_recv)
-        for relay, comes in relays:
-            pl.when(comes)(relay.wait_recv)
         ghosts = []
         for face in range(6):
-            direction, slot = face % 2, face // 2
-            at = jnp.broadcast_to(where_at[face : face + 1, :], (8, lanes))
-            is_packed = odd == direction
-            at_high = jnp.where(is_packed, jnp.minimum(at + half, lanes - 1), at)
-            hops = jnp.broadcast_to(hop_of[face : face + 1, :], (8, lanes))
-            pieces = []
-            for r in range(0, area, 8):
-                row = slot * area + r
-                block = jnp.zeros((8, lanes), F32)
-                for hop in range(HOPS + 1):
-                    index = at
-                    if hop == 0:
-                        window = faces[direction, pl.ds(row, 8), :]
-                    elif hop < HOPS or row < pack:
-                        window = windows[direction, hop - 1, pl.ds(row, 8), :]
-                    else:
-                        start = pl.multiple_of(row - jnp.where(is_packed, pack, 0), 8)
-                        window = windows[direction, hop - 1, pl.ds(start, 8), :]
-                        index = at_high
-                    block = jnp.where(hops == hop, pick(window, index), block)
-                pieces.append(block)
-            ghosts.append(jnp.concatenate(pieces, axis=0))
+            relay, comes = relays[face]
+            pl.when(comes)(relay.wait_recv)
+            blocks = [held[face, pl.ds(r, 8), :] for r in range(0, area, 8)]
+            ghosts.append(jnp.concatenate(ghost(face, (1, 2, 3), blocks), axis=0))
         return ghosts
 
     zrow = lax.broadcasted_iota(jnp.int32, (8, 8, lanes), 1)
+
+    zghost[...] = jnp.zeros_like(zghost)
+
+    def inner(values):
+        for x in range(8):
+            rows = pl.ds(64 * x, 64)
+            here = values[rows, :]
+            edge = jnp.zeros((8, lanes), F32)
+            beside = jnp.concatenate([edge, here[:-8]], axis=0) + jnp.concatenate(
+                [here[8:], edge], axis=0
+            )
+            if x > 0:
+                beside = beside + values[pl.ds(64 * (x - 1), 64), :]
+            if x < 7:
+                beside = beside + values[pl.ds(64 * (x + 1), 64), :]
+            cube = here.reshape(8, 8, lanes)
+            below = jnp.where(zrow == 0, 0.0, pltpu.roll(cube, 1, 1))
+            above = jnp.where(zrow == 7, 0.0, pltpu.roll(cube, 7, 1))
+            beside = beside + (below + above).reshape(64, lanes)
+            applied_ref[rows, :] = 6.0 * here - beside
 
     def fine(values, ghosts, use):
         g0, g1, g2, g3, g4, g5 = ghosts
@@ -217,27 +248,41 @@
         zghost[pl.ds(7, 64, 8), :] = g5
         for x in range(8):
             rows = pl.ds(64 * x, 64)
-            here = values[rows, :]
-            beside = (g0 if x == 0 else values[pl.ds(64 * (x - 1), 64), :]) + (
-                g1 if x == 7 else values[pl.ds(64 * (x + 1), 64), :]
+            applied = applied_ref[rows, :] - zghost[rows, :]
+            if x == 0:
+                applied = applied - g0
+            if x == 7:
+                applied = applied - g1
+            applied = jnp.concatenate(
+                [
+                    applied[:8] - g2[8 * x : 8 * x + 8],
+                    applied[8:56],
+                    applied[56:] - g3[8 * x : 8 * x + 8],
+                ],
+                axis=0,
             )
-            beside = beside + jnp.concatenate([g2[8 * x : 8 * x + 8], here[:-8]], axis=0)
-            beside = beside + jnp.concatenate([here[8:], g3[8 * x : 8 * x + 8]], axis=0)
-            cube = here.reshape(8, 8, lanes)
-            edge = zghost[rows, :].reshape(8, 8, lanes)
-            below = jnp.where(zrow == 0, edge, pltpu.roll(cube, 1, 1))
-            above = jnp.where(zrow == 7, edge, pltpu.roll(cube, 7, 1))
-            beside = beside + (below + above).reshape(64, lanes)
-            use(x, rows, here, 6.0 * here - beside)
+            use(x, rows, values[rows, :], applied)
 
     def exchange_fine(stage, k, values):
         return exchange(
-            stage, values, 8, faces_fine.at[k], packed_fine.at[k], windows_fine.at[k]
+            stage,
+            values,
+            8,
+            faces_fine.at[k],
+            packed_fine.at[k],
+            windows_fine.at[k],
+            lambda: inner(values),
         )
 
-    def exchange_coarse(stage, k):
+    def exchange_coarse(stage, k, meanwhile):
         return exchange(
-            stage, coarse, 4, faces_coarse.at[k], packed_coarse.at[k], windows_coarse.at[k]
+            stage,
+            coarse,
+            4,
+            faces_coarse.at[k],
+            packed_coarse.at[k],
+            windows_coarse.at[k],
+            meanwhile,
         )
 
     def sweep(x, rows, here, applied):
@@ -261,7 +306,7 @@
     coarse_rhs = 0.125 * (paired[pl.ds(0, 64, 2), :] + paired[pl.ds(1, 64, 2), :])
     coarse_one = RELAX_COARSE * coarse_rhs
     coarse[...] = coarse_one
-    g0, g1, g2, g3, g4, g5 = exchange_coarse(2, 0)
+    g0, g1, g2, g3, g4, g5 = exchange_coarse(2, 0, lambda: None)
     beside = jnp.concatenate([g0, coarse_one[:-16]], axis=0) + jnp.concatenate(
         [coarse_one[16:], g1], axis=0
     )
@@ -280,12 +325,16 @@
     coarse[...] = coarse_two
     paired[pl.ds(0, 64, 2), :] = coarse_two
     paired[pl.ds(1, 64, 2), :] = coarse_two
-    for x in range(8):
-        for y in range(8):
-            rows = pl.ds(64 * x + 8 * y, 8)
-            second[rows, :] = second[rows, :] + paired[pl.ds(32 * (x // 2) + 8 * (y // 2), 8), :]
-
-    corrections = exchange_coarse(3, 1)
+
+    def correct():
+        for x in range(8):
+            for y in range(8):
+                rows = pl.ds(64 * x + 8 * y, 8)
+                lift = paired[pl.ds(32 * (x // 2) + 8 * (y // 2), 8), :]
+                second[rows, :] = second[rows, :] + lift
+        inner(second)
+
+    corrections = exchange_coarse(3, 1, correct)
     for face in range(6):
         doubled[face, pl.ds(0, 16, 2), :] = corrections[face]
         doubled[face, pl.ds(1, 16, 2), :] = corrections[face]
@@ -311,10 +360,10 @@
 
     fine(first, exchange_fine(4, 2, first), finish)
 
-    row = lax.broadcasted_iota(jnp.int32, (8, lanes), 0)
-    tile = jnp.zeros((8, lanes), F32)
+    tile = jnp.zeros((1, lanes), F32)
     for k in range(5):
-        tile = jnp.where(row == k, jnp.sum(parts[k], axis=0, keepdims=True), tile)
+        one = jnp.sum(jnp.sum(parts[k], axis=0, keepdims=True), axis=1, keepdims=True)
+        tile = jnp.where(lane == k, one, tile)
     base = 0
     for size, mine, peer in stages:
         sums[base + mine] = tile
@@ -336,11 +385,12 @@
         for made in copies:
             made.wait_send()
         base += size
-    whole = jnp.sum(tile, axis=1, keepdims=True)
-    along, curvature, old_square, cross, image_square = [whole[k : k + 1] for k in range(5)]
+    along, curvature, old_square, cross, image_square = [
+        jnp.sum(jnp.where(lane == k, tile, 0.0), axis=1, keepdims=True) for k in range(5)
+    ]
     step = along / curvature
     square = old_square - 2.0 * step * cross + step * step * image_square
-    norm_ref[...] = jnp.broadcast_to(jnp.sqrt(square), norm_ref.shape)
+    norm_ref[0] = jnp.sqrt(square)[0, 0]
     for x in range(8):
         rows = pl.ds(64 * x, 64)
         solution_ref[rows, :] = step * first[rows, :]
@@ -379,9 +429,9 @@
     block = jax.ShapeDtypeStruct((cells, lanes), F32)
     out = pl.pallas_call(
         body,
-        out_shape=(block, block, jax.ShapeDtypeStruct((8, lanes), F32)),
+        out_shape=(block, block, jax.ShapeDtypeStruct((1,), F32)),
         in_specs=[vmem, pl.BlockSpec(memory_space=pltpu.SMEM), vmem],
-        out_specs=(vmem, vmem, vmem),
+        out_specs=(vmem, vmem, pl.BlockSpec(memory_space=pltpu.SMEM)),
         scratch_shapes=[
             pltpu.VMEM((cells, lanes), F32),
             pltpu.VMEM((cells, lanes), F32),
@@ -392,13 +442,15 @@
             pltpu.VMEM((cells // 8, lanes), F32),
             pltpu.VMEM((4, cells // 8, lanes), F32),
             pltpu.VMEM((6, 32, lanes), F32),
+            pltpu.VMEM((6, 64, lanes), F32),
+            pltpu.VMEM((cells, lanes), F32),
             pltpu.VMEM((3, 2, 192, lanes), F32),
             pltpu.VMEM((3, 96, lanes), F32),
             pltpu.VMEM((3, 2, HOPS, 192, lanes), F32),
             pltpu.VMEM((2, 2, 48, lanes), F32),
             pltpu.VMEM((2, 24, lanes), F32),
             pltpu.VMEM((2, 2, HOPS, 48, lanes), F32),
-            pltpu.VMEM((sum_rows, 8, lanes), F32),
+            pltpu.VMEM((sum_rows, 1, lanes), F32),
             pltpu.SemaphoreType.DMA((5, 2, 3)),
             pltpu.SemaphoreType.DMA((5, 2, 3)),
             pltpu.SemaphoreType.DMA((5, 2, 3)),
@@ -412,7 +464,7 @@
         ],
         compiler_params=pltpu.CompilerParams(collective_id=0, has_side_effects=True),
     )(right_side, counts, neighbours)
-    return out[0], out[1], out[2][0, 0]
+    return out[0], out[1], out[2].reshape(())
 
 
 def solution(mesh):

time: 50 us -> 49.2 us (0.984)
  between operations: 0.64 us -> 2.41 us
  Pallas kernels: 45.6 us -> 44.2 us
  local copies, waits for them, and re-layouts: 3.61 us -> 2.42 us
    pallas_call x1, Pallas kernels: 45.6 us -> 44.2 us  [local(): pl.pallas_call(body, out_shape=(block, block, jax.ShapeDtypeStruct((1,),...]
    slice x1 -> x0, local copies, waits for them, and re-layouts: 1.19 us -> none  [local(): return (out[0], out[1], out[2][0, 0])]
where the time goes in v4:
time: 49.2 us; the launch traced here: 49 us
  Pallas kernels  44.2 us (90%)
  local copies, waits for them, and re-layouts  2.42 us (5%)
  between operations  2.41 us (5%)
    pallas_call x1, Pallas kernels, local(): pl.pallas_call(body, out_shape=(block, block, jax.ShapeDtypeStruct((1,),...  44.2 us
    unnamed x4, local copies, waits for them, and re-layouts  2.42 us

profile of v4, /device:TPU:0, one launch (start us, length us, event | category | flops | bytes accessed | tf_op | source)
XLA Modules:
  0.0 49.0 jit_solution(3298402295431870543)
XLA Ops:
  0.6 44.2 %shard_map.58 = (f32[512,128]{1,0:T(8,128)}, f32[512,128]{1,0:T(8,128)}, f32[1]{0:T(128)}) custom-call(f32[512,128]{1,0:T(8,128)} %refs_0_.1, s32[32]{0:T(128)} %refs_1_.1, s32[6,128]{1,0:T(8,128)} %refs_2_.1), custom_call_target="tpu_custom_call" | custom-call | tf_op jit(solution)/shard_map/pallas_call | solution.py:430
  44.8 0.0 copy-start
  44.8 1.7 %copy.9 = f32[512,128]{1,0:T(8,128)} copy(f32[512,128]{1,0:T(8,128)} %get-tuple-element.12) | data formatting | bytes 524288
  46.5 0.0 copy-done
  46.5 0.7 %copy.10 = f32[512,128]{1,0:T(8,128)} copy(f32[512,128]{1,0:T(8,128)S(1)} %copy-done) | data formatting | bytes 524288
Async XLA Ops:
  44.8 1.7 %copy-start = (f32[512,128]{1,0:T(8,128)S(1)}, f32[512,128]{1,0:T(8,128)}, u32[]{:S(2)}) copy-start(f32[512,128]{1,0:T(8,128)} %get-tuple-element.13) | copy-start | bytes 786436
